TPU v7x, 256 devices: a whole 4x4x8 slice. The times are simulated.
256 devices in a mesh: dp: 4 (over y), space: 64 (over x, z, core).
Axes of the slice: x: 4, y: 4, z: 8, core: 2. Of those that a mesh axis runs over, the one named last changes fastest.
Arguments:
- queries: bfloat16 [32, 200, 256], P('dp'), may hold values from -6 to 6
- query_pos: bfloat16 [200, 256], replicated, may hold values from -6 to 6
- pixels: bfloat16 [32, 16384, 256], P('dp', 'space'), may hold values from -160 to 160
- pixel_pos: bfloat16 [16384, 256], P('space'), may hold values from -6 to 6
- masks: int32 [32, 200, 16384], P('dp', None, 'space'), may hold values from 0 to 1, as said below
- wq_cross: bfloat16 [256, 256], replicated, may hold values from -0.375 to 0.375
- wk_cross: bfloat16 [256, 256], replicated, may hold values from -0.375 to 0.375
- wv_cross: bfloat16 [256, 256], replicated, may hold values from -0.375 to 0.375
- wo_cross: bfloat16 [256, 256], replicated, may hold values from -0.375 to 0.375
- gain_cross: float32 [256], replicated, may hold values from 0.1 to 1.9
- w_qkv: bfloat16 [256, 768], replicated, may hold values from -0.375 to 0.375
- wo_self: bfloat16 [256, 256], replicated, may hold values from -0.375 to 0.375
- gain_self: float32 [256], replicated, may hold values from 0.1 to 1.9
- w_in: bfloat16 [256, 2048], replicated, may hold values from -0.375 to 0.375
- w_out: bfloat16 [2048, 256], replicated, may hold values from -0.125 to 0.125
- gain_ffn: float32 [256], replicated, may hold values from 0.1 to 1.9
Outputs:
- new_queries: bfloat16 [32, 200, 256], P('dp')
Inputs may be any that keep to these rules, and one draw needn't show every extreme that they name: `masks`: 0 or 1; each row's ones lie within a run of at most 768 consecutive pixels, which may lie anywhere in the image; a row may have no ones on some devices' pixels or on all pixels of its image.
All inputs are finite; a program needn't handle non-finite values.
Results may differ from a plain program's by a relative error of at most 0.017.
The roundings to bfloat16 on the way count: a program that leaves them out, or rounds other values in their place, can miss the bound.
Values may be sent and summed in bfloat16 or wider, within the bound.
A program may use at most 128 MiB of HBM per device.

v0:
```python
import math

import jax
import jax.numpy as jnp
from jax import lax
from jax.experimental import pallas as pl
from jax.experimental.pallas import tpu as pltpu
from jax.sharding import PartitionSpec as P

HEADS = 8
HEAD = 32
NX = 4
NZ = 8
LANES = 256
FAR = -1e30
MESH = pl.DeviceIdType.MESH
F32 = jnp.float32
BF16 = jnp.bfloat16


def dot(a, b, contract=((1,), (0,))):
    return lax.dot_general(a, b, (contract, ((), ())), preferred_element_type=F32)


def dot_nt(a, b):
    return dot(a, b, ((1,), (1,)))


def layer_norm(x, gain):
    mean = jnp.mean(x, axis=-1, keepdims=True)
    d = x - mean
    var = jnp.mean(d * d, axis=-1, keepdims=True)
    return d / jnp.sqrt(var + 1e-05) * gain


def merge(tops, totals):
    most = totals[0]
    for t in totals[1:]:
        most = jnp.maximum(most, t)
    some = most > 0
    seen = [jnp.where(some & (t < 0), -3e38, m) for m, t in zip(tops, totals)]
    top = seen[0]
    for m in seen[1:]:
        top = jnp.maximum(top, m)
    scales = [jnp.exp2(m - top) for m in seen]
    total = scales[0] * jnp.abs(totals[0])
    for s, t in zip(scales[1:], totals[1:]):
        total = total + s * jnp.abs(t)
    return top, jnp.where(some, total, -total), scales


def kernel(
    queries, query_pos, pixels, pixel_pos, masks, wq, wk, wv, wo, gain_cross, w_qkv, wo_self, gain_self, w_in, w_out,
    gain_ffn,
    out,
    wq_t, wv_t, eye, keys, values_t, query_t, bias, own_o, own_m,
    p1o, p1m, r1o, r1m, p2o, p2m, r2o, r2m, p3o, p3m, r3o, r3m, att,
    s1, v1, s2, v2, s3, v3, s4, v4, s5, v5, s6, v6,
):
    nq = queries.shape[1]
    width = queries.shape[2]
    pix = pixels.shape[1]
    me = lax.axis_index("space")
    core = lax.rem(me, 2)
    z = lax.rem(me // 2, NZ)
    x = me // (2 * NZ)
    factor = math.log2(math.e) / math.sqrt(HEAD)

    def at(xx, zz, cc):
        return {"space": (xx * NZ + zz) * 2 + cc}

    def x_peer(d):
        return at(lax.rem(x + d, NX), z, core)

    def z_peer(d):
        return at(x, lax.rem(z + d, NZ), core)

    partner = at(x, z, 1 - core)

    barrier = pltpu.get_barrier_semaphore()
    pl.semaphore_signal(barrier, inc=1, device_id=partner, device_id_type=MESH)
    for d in range(1, NX):
        pl.semaphore_signal(barrier, inc=1, device_id=x_peer(d), device_id_type=MESH)
    for d in range(1, NZ):
        pl.semaphore_signal(barrier, inc=1, device_id=z_peer(d), device_id_type=MESH)

    def send(src, dst, send_sem, recv_sem, where):
        return pltpu.make_async_remote_copy(
            src_ref=src, dst_ref=dst, send_sem=send_sem, recv_sem=recv_sem, device_id=where, device_id_type=MESH
        )

    rows = lax.broadcasted_iota(jnp.int32, (pix, pix), 0)
    cols = lax.broadcasted_iota(jnp.int32, (pix, pix), 1)
    eye[...] = jnp.where(rows == cols, 1.0, 0.0).astype(BF16)
    wq_t[...] = dot_nt(eye[...], wq[...]).astype(BF16)
    wv_t[...] = dot_nt(eye[...], wv[...]).astype(BF16)
    query_t[...] = jnp.zeros_like(query_t)
    bias[...] = jnp.zeros_like(bias)
    for h in range(HEADS):
        values_t[h, HEAD:, :] = jnp.ones((16, pix), BF16)

    def partial(i, put_o, m_ref):
        one = pixels[i]
        key_in = (one.astype(F32) + pixel_pos[...].astype(F32)).astype(BF16)
        keys[...] = dot(key_in, wk[...]).astype(BF16)
        v_t = dot_nt(wv_t[...], one).astype(BF16)
        for h in range(HEADS):
            values_t[h, :HEAD, :] = v_t[h * HEAD : (h + 1) * HEAD, :]
        query_in = (queries[i].astype(F32) + query_pos[...].astype(F32)).astype(BF16)
        query_t[:, :nq] = dot_nt(wq_t[...], query_in).astype(BF16)
        mask_t = dot_nt(eye[...], masks[i].astype(F32).astype(BF16))
        count = jnp.sum(mask_t, axis=0, keepdims=True)
        bias[:, :nq] = jnp.where((mask_t > 0.5) | (count == 0.0), 0.0, FAR)
        sign = jnp.where(count == 0.0, -1.0, 1.0)
        for h in range(HEADS):
            tile = (h // 4) * 128
            lane = (h % 4) * HEAD
            parts = []
            if lane:
                parts.append(jnp.zeros((lane, LANES), BF16))
            parts.append(query_t[h * HEAD : (h + 1) * HEAD, :])
            if lane + HEAD < 128:
                parts.append(jnp.zeros((128 - lane - HEAD, LANES), BF16))
            one_head = jnp.concatenate(parts, axis=0)
            score = dot(keys[:, tile : tile + 128], one_head) * factor + bias[...]
            top = jnp.max(score, axis=0, keepdims=True)
            weight = jnp.exp2(score - top).astype(BF16)
            both = dot(values_t[h], weight)
            put_o(h, both[:HEAD])
            m_ref[h : h + 1, :] = top
            m_ref[HEADS + h : HEADS + h + 1, :] = both[HEAD : HEAD + 1]
        m_ref[HEADS:, :nq] = m_ref[HEADS:, :nq] * sign

    def first(j, carry):
        i = (1 - core) * NX + lax.rem(x + j + 1, NX)

        def put(h, value):
            p1o[j, h * HEAD : (h + 1) * HEAD, :] = value.astype(BF16)

        partial(i, put, p1m.at[j])

        @pl.when(j == 0)
        def _():
            pl.semaphore_wait(barrier, NX + NZ - 1)

        send(p1o.at[j], r1o.at[j], s1.at[j, 0], v1.at[j, 0], partner).start()
        send(p1m.at[j], r1m.at[j], s1.at[j, 1], v1.at[j, 1], partner).start()
        return carry

    lax.fori_loop(0, NX, first, 0)

    def second(j, carry):
        i = core * NX + lax.rem(x + j + 1, NX)

        def put(h, value):
            own_o[h * HEAD : (h + 1) * HEAD, :] = value

        partial(i, put, own_m)
        a = send(p1o.at[j], r1o.at[j], s1.at[j, 0], v1.at[j, 0], partner)
        b = send(p1m.at[j], r1m.at[j], s1.at[j, 1], v1.at[j, 1], partner)
        a.wait()
        b.wait()
        top, total, scales = merge([own_m[:HEADS], r1m[j, :HEADS]], [own_m[HEADS:], r1m[j, HEADS:]])
        p2m[j, :HEADS] = top
        p2m[j, HEADS:] = total
        for h in range(HEADS):
            part = slice(h * HEAD, (h + 1) * HEAD)
            folded = own_o[part] * scales[0][h : h + 1] + r1o[j, part].astype(F32) * scales[1][h : h + 1]
            p2o[j, part] = folded.astype(BF16)

        @pl.when(j < NX - 1)
        def _():
            to = x_peer(j + 1)
            send(p2o.at[j], r2o.at[j], s2.at[j, 0], v2.at[j, 0], to).start()
            send(p2m.at[j], r2m.at[j], s2.at[j, 1], v2.at[j, 1], to).start()

        return carry

    lax.fori_loop(0, NX, second, 0)

    mine = NX - 1
    for j in range(NX - 1):
        to = x_peer(j + 1)
        send(p2o.at[j], r2o.at[j], s2.at[j, 0], v2.at[j, 0], to).wait()
        send(p2m.at[j], r2m.at[j], s2.at[j, 1], v2.at[j, 1], to).wait()
    tops = [p2m[mine, :HEADS]] + [r2m[j, :HEADS] for j in range(NX - 1)]
    totals = [p2m[mine, HEADS:]] + [r2m[j, HEADS:] for j in range(NX - 1)]
    top, total, scales = merge(tops, totals)
    for h in range(HEADS):
        part = slice(h * HEAD, (h + 1) * HEAD)
        folded = p2o[mine, part].astype(F32) * scales[0][h : h + 1]
        for j in range(NX - 1):
            folded = folded + r2o[j, part].astype(F32) * scales[j + 1][h : h + 1]
        p3o[h] = folded.astype(BF16)
        p3m[h, 0:1] = top[h : h + 1]
        p3m[h, 1:2] = total[h : h + 1]

    def z_send(d):
        h = lax.rem(z + d, NZ)
        return (
            send(p3o.at[h], r3o.at[d - 1], s3.at[d - 1, 0], v3.at[d - 1, 0], z_peer(d)),
            send(p3m.at[h], r3m.at[d - 1], s3.at[d - 1, 1], v3.at[d - 1, 1], z_peer(d)),
        )

    order = (4, 3, 5, 2, 6, 1, 7)
    for d in order:
        for copy in z_send(d):
            copy.start()
    for d in order[::-1]:
        for copy in z_send(d):
            copy.wait()
    tops = [p3m[z, 0:1]] + [r3m[d, 0:1] for d in range(NZ - 1)]
    totals = [p3m[z, 1:2]] + [r3m[d, 1:2] for d in range(NZ - 1)]
    top, total, scales = merge(tops, totals)
    folded = p3o[z].astype(F32) * scales[0]
    for d in range(NZ - 1):
        folded = folded + r3o[d].astype(F32) * scales[d + 1]
    att[z] = (folded / jnp.abs(total)).astype(BF16)

    def z_gather(d):
        return send(att.at[z], att.at[z], s4.at[d - 1], v4.at[d - 1], z_peer(d))

    for d in order:
        z_gather(d).start()
    for d in order[::-1]:
        z_gather(d).wait()

    i_own = core * NX + x
    attended_t = att[...].reshape(width, LANES)
    cross = dot(attended_t, wo[...], ((0,), (0,)))[:nq]
    pos = query_pos[...].astype(F32)
    after_cross = layer_norm(queries[i_own].astype(F32) + cross, gain_cross[...]).astype(BF16)
    self_in = (after_cross.astype(F32) + pos).astype(BF16)
    both = dot(self_in, w_qkv[:, : 2 * width]).astype(BF16)
    self_v = dot(after_cross, w_qkv[:, 2 * width :]).astype(BF16)
    head_of = lax.broadcasted_iota(jnp.int32, (nq, 128), 1) // HEAD
    outs = []
    for tile in range(width // 128):
        part = slice(tile * 128, (tile + 1) * 128)
        q_tile = both[:, part].astype(F32)
        k_tile = both[:, width + tile * 128 : width + (tile + 1) * 128]
        v_tile = self_v[:, part]
        gathered = jnp.zeros((nq, 128), F32)
        for h in range(128 // HEAD):
            q_head = jnp.where(head_of == h, q_tile, 0.0).astype(BF16)
            logits = dot_nt(q_head, k_tile) * (1.0 / math.sqrt(HEAD))
            top = jnp.max(logits, axis=-1, keepdims=True)
            expo = jnp.exp(logits - top)
            weight = (expo / jnp.sum(expo, axis=-1, keepdims=True)).astype(BF16)
            gathered = jnp.where(head_of == h, dot(weight, v_tile), gathered)
        outs.append(gathered.astype(BF16))
    self_proj = dot(jnp.concatenate(outs, axis=1), wo_self[...])
    after_self = layer_norm(after_cross.astype(F32) + self_proj, gain_self[...]).astype(BF16)
    hidden = jnp.maximum(dot(after_self, w_in[...]), 0.0).astype(BF16)
    ffn = dot(hidden, w_out[...])
    out[i_own] = layer_norm(after_self.astype(F32) + ffn, gain_ffn[...]).astype(BF16)

    def x_out(d):
        return send(out.at[i_own], out.at[i_own], s5.at[d - 1], v5.at[d - 1], x_peer(d))

    def core_out(k):
        i = core * NX + lax.rem(x - k + NX, NX)
        return send(out.at[i], out.at[i], s6.at[k], v6.at[k], partner)

    for d in (2, 1, 3):
        x_out(d).start()
    core_out(0).start()
    for d in (1, 3, 2):
        x_out(d).wait_recv()
        core_out(d).start()
    for d in (1, 2, 3):
        x_out(d).wait_send()
    for k in range(NX):
        core_out(k).wait()


def local(
    queries, query_pos, pixels, pixel_pos, masks, wq_cross, wk_cross, wv_cross, wo_cross, gain_cross, w_qkv, wo_self,
    gain_self, w_in, w_out, gain_ffn,
):
    images, nq, width = queries.shape
    pix = pixels.shape[1]
    dma = pltpu.SemaphoreType.DMA
    vmem = pltpu.VMEM
    scratch = [
        vmem((width, width), BF16),
        vmem((width, width), BF16),
        vmem((pix, pix), BF16),
        vmem((pix, width), BF16),
        vmem((HEADS, HEAD + 16, pix), BF16),
        vmem((width, LANES), BF16),
        vmem((pix, LANES), F32),
        vmem((width, LANES), F32),
        vmem((2 * HEADS, LANES), F32),
        vmem((NX, width, LANES), BF16),
        vmem((NX, 2 * HEADS, LANES), F32),
        vmem((NX, width, LANES), BF16),
        vmem((NX, 2 * HEADS, LANES), F32),
        vmem((NX, width, LANES), BF16),
        vmem((NX, 2 * HEADS, LANES), F32),
        vmem((NX - 1, width, LANES), BF16),
        vmem((NX - 1, 2 * HEADS, LANES), F32),
        vmem((NZ, HEAD, LANES), BF16),
        vmem((NZ, 8, LANES), F32),
        vmem((NZ - 1, HEAD, LANES), BF16),
        vmem((NZ - 1, 8, LANES), F32),
        vmem((NZ, HEAD, LANES), BF16),
        dma((NX, 2)),
        dma((NX, 2)),
        dma((NX - 1, 2)),
        dma((NX - 1, 2)),
        dma((NZ - 1, 2)),
        dma((NZ - 1, 2)),
        dma((NZ - 1,)),
        dma((NZ - 1,)),
        dma((NX - 1,)),
        dma((NX - 1,)),
        dma((NX,)),
        dma((NX,)),
    ]
    return pl.pallas_call(
        kernel,
        out_shape=jax.ShapeDtypeStruct((images, nq, width), BF16),
        in_specs=[pl.BlockSpec(memory_space=pltpu.VMEM)] * 16,
        out_specs=pl.BlockSpec(memory_space=pltpu.VMEM),
        scratch_shapes=scratch,
        compiler_params=pltpu.CompilerParams(
            collective_id=0, has_side_effects=True, vmem_limit_bytes=48 * 1024 * 1024
        ),
        name="decoder_layer",
    )(
        queries, query_pos, pixels, pixel_pos, masks, wq_cross, wk_cross, wv_cross, wo_cross, gain_cross[None], w_qkv,
        wo_self, gain_self[None], w_in, w_out, gain_ffn[None],
    )


def solution(mesh):
    placed = (
        P("dp", None, None),
        P(),
        P("dp", "space", None),
        P("space", None),
        P("dp", None, "space"),
    ) + (P(),) * 11
    return jax.shard_map(local, mesh=mesh, in_specs=placed, out_specs=P("dp", None, None), check_vma=False)
```

profile of v0, /device:TPU:1, one launch (start us, length us, event | category | flops | bytes accessed | tf_op | source)
XLA Modules:
  0.0 68.8 jit_solution(9079405510330491837)
XLA Ops:
  0.0 0.0 copy-start
  0.0 1.2 %copy-done = bf16[8,256,256]{2,1,0:T(8,128)(2,1)S(1)} copy-done((bf16[8,256,256]{2,1,0:T(8,128)(2,1)S(1)}, bf16[8,256,256]{2,1,0:T(8,128)(2,1)}, u32[]{:S(2)}) %copy-start) | copy-done | bytes 1048600
  1.2 0.0 copy-start.1
  1.2 1.2 %copy-done.1 = bf16[256,2048]{1,0:T(8,128)(2,1)S(1)} copy-done((bf16[256,2048]{1,0:T(8,128)(2,1)S(1)}, bf16[256,2048]{1,0:T(8,128)(2,1)}, u32[]{:S(2)}) %copy-start.1) | copy-done | bytes 1048600
  2.5 0.0 copy-start.2
  2.5 1.2 %copy-done.2 = bf16[2048,256]{1,0:T(8,128)(2,1)S(1)} copy-done((bf16[2048,256]{1,0:T(8,128)(2,1)S(1)}, bf16[2048,256]{1,0:T(8,128)(2,1)}, u32[]{:S(2)}) %copy-start.2) | copy-done | bytes 1048600
  3.7 0.0 copy-start.3
  3.7 1.1 %copy-done.3 = bf16[8,200,256]{2,1,0:T(8,128)(2,1)S(1)} copy-done((bf16[8,200,256]{2,1,0:T(8,128)(2,1)S(1)}, bf16[8,200,256]{2,1,0:T(8,128)(2,1)}, u32[]{:S(2)}) %copy-start.3) | copy-done | bytes 819224
  4.8 0.0 copy-start.4
  4.8 1.0 %copy-done.4 = bf16[256,768]{1,0:T(8,128)(2,1)S(1)} copy-done((bf16[256,768]{1,0:T(8,128)(2,1)S(1)}, bf16[256,768]{1,0:T(8,128)(2,1)}, u32[]{:S(2)}) %copy-start.4) | copy-done | bytes 393240
  5.8 0.0 copy-start.5
  5.8 0.9 %copy-done.5 = bf16[256,256]{1,0:T(8,128)(2,1)S(1)} copy-done((bf16[256,256]{1,0:T(8,128)(2,1)S(1)}, bf16[256,256]{1,0:T(8,128)(2,1)}, u32[]{:S(2)}) %copy-start.5) | copy-done | bytes 131096
  6.7 0.0 copy-start.6
  6.7 0.9 %copy-done.6 = bf16[256,256]{1,0:T(8,128)(2,1)S(1)} copy-done((bf16[256,256]{1,0:T(8,128)(2,1)S(1)}, bf16[256,256]{1,0:T(8,128)(2,1)}, u32[]{:S(2)}) %copy-start.6) | copy-done | bytes 131096
  7.6 0.0 copy-start.7
  7.6 0.9 %copy-done.7 = bf16[256,256]{1,0:T(8,128)(2,1)S(1)} copy-done((bf16[256,256]{1,0:T(8,128)(2,1)S(1)}, bf16[256,256]{1,0:T(8,128)(2,1)}, u32[]{:S(2)}) %copy-start.7) | copy-done | bytes 131096
  8.5 0.0 copy-start.8
  8.5 0.9 %copy-done.8 = bf16[256,256]{1,0:T(8,128)(2,1)S(1)} copy-done((bf16[256,256]{1,0:T(8,128)(2,1)S(1)}, bf16[256,256]{1,0:T(8,128)(2,1)}, u32[]{:S(2)}) %copy-start.8) | copy-done | bytes 131096
  9.4 0.0 copy-start.9
  9.4 0.9 %copy-done.9 = bf16[256,256]{1,0:T(8,128)(2,1)S(1)} copy-done((bf16[256,256]{1,0:T(8,128)(2,1)S(1)}, bf16[256,256]{1,0:T(8,128)(2,1)}, u32[]{:S(2)}) %copy-start.9) | copy-done | bytes 131096
  10.3 0.0 copy-start.10
  10.3 0.9 %copy-done.10 = bf16[256,256]{1,0:T(8,128)(2,1)S(1)} copy-done((bf16[256,256]{1,0:T(8,128)(2,1)S(1)}, bf16[256,256]{1,0:T(8,128)(2,1)}, u32[]{:S(2)}) %copy-start.10) | copy-done | bytes 131096
  11.2 0.0 copy-start.11
  11.2 0.9 %copy-done.11 = bf16[200,256]{1,0:T(8,128)(2,1)S(1)} copy-done((bf16[200,256]{1,0:T(8,128)(2,1)S(1)}, bf16[200,256]{1,0:T(8,128)(2,1)}, u32[]{:S(2)}) %copy-start.11) | copy-done | bytes 102424
  12.1 0.0 copy-start.12
  12.1 0.7 copy-done.12
  12.8 0.0 copy-start.13
  12.8 0.7 copy-done.13
  13.5 0.0 copy-start.14
  13.5 0.7 copy-done.14
  14.2 53.7 %decoder_layer.1 = bf16[8,200,256]{2,1,0:T(8,128)(2,1)S(1)} custom-call(bf16[8,200,256]{2,1,0:T(8,128)(2,1)S(1)} %copy-done.3, bf16[200,256]{1,0:T(8,128)(2,1)S(1)} %copy-done.11, bf16[8,256,256]{2,1,0:T(8,128)(2,1)S(1)} %copy-done, bf16[256,256]{1,0:T(8,128)(2,1)S(1)} %copy-done.5, s32[8,200,256]{2,1,0:T(8,128)} %masks.1, bf16[256,256]{1,0:T(8,128)(2,1)S(1)} %copy-done.6, ...), custom_call_target="tpu_custom_call" | custom-call | tf_op jit(solution)/shard_map/decoder_layer/pallas_call | solution.py:321
  67.9 0.9 %copy.18 = bf16[8,200,256]{2,1,0:T(8,128)(2,1)} copy(bf16[8,200,256]{2,1,0:T(8,128)(2,1)S(1)} %decoder_layer.1) | data formatting | bytes 1638400
Async XLA Ops:
  0.0 1.2 %copy-start = (bf16[8,256,256]{2,1,0:T(8,128)(2,1)S(1)}, bf16[8,256,256]{2,1,0:T(8,128)(2,1)}, u32[]{:S(2)}) copy-start(bf16[8,256,256]{2,1,0:T(8,128)(2,1)} %pixels.1) | copy-start | bytes 3145732
  1.2 1.2 %copy-start.1 = (bf16[256,2048]{1,0:T(8,128)(2,1)S(1)}, bf16[256,2048]{1,0:T(8,128)(2,1)}, u32[]{:S(2)}) copy-start(bf16[256,2048]{1,0:T(8,128)(2,1)} %w_in.1) | copy-start | bytes 3145732
  2.5 1.2 %copy-start.2 = (bf16[2048,256]{1,0:T(8,128)(2,1)S(1)}, bf16[2048,256]{1,0:T(8,128)(2,1)}, u32[]{:S(2)}) copy-start(bf16[2048,256]{1,0:T(8,128)(2,1)} %w_out.1) | copy-start | bytes 3145732
  3.7 1.1 %copy-start.3 = (bf16[8,200,256]{2,1,0:T(8,128)(2,1)S(1)}, bf16[8,200,256]{2,1,0:T(8,128)(2,1)}, u32[]{:S(2)}) copy-start(bf16[8,200,256]{2,1,0:T(8,128)(2,1)} %queries.1) | copy-start | bytes 2457604
  4.8 1.0 %copy-start.4 = (bf16[256,768]{1,0:T(8,128)(2,1)S(1)}, bf16[256,768]{1,0:T(8,128)(2,1)}, u32[]{:S(2)}) copy-start(bf16[256,768]{1,0:T(8,128)(2,1)} %w_qkv.1) | copy-start | bytes 1179652
  5.8 0.9 %copy-start.5 = (bf16[256,256]{1,0:T(8,128)(2,1)S(1)}, bf16[256,256]{1,0:T(8,128)(2,1)}, u32[]{:S(2)}) copy-start(bf16[256,256]{1,0:T(8,128)(2,1)} %pixel_pos.1) | copy-start | bytes 393220
  6.7 0.9 %copy-start.6 = (bf16[256,256]{1,0:T(8,128)(2,1)S(1)}, bf16[256,256]{1,0:T(8,128)(2,1)}, u32[]{:S(2)}) copy-start(bf16[256,256]{1,0:T(8,128)(2,1)} %wq.1) | copy-start | bytes 393220
  7.6 0.9 %copy-start.7 = (bf16[256,256]{1,0:T(8,128)(2,1)S(1)}, bf16[256,256]{1,0:T(8,128)(2,1)}, u32[]{:S(2)}) copy-start(bf16[256,256]{1,0:T(8,128)(2,1)} %wk.1) | copy-start | bytes 393220
  8.5 0.9 %copy-start.8 = (bf16[256,256]{1,0:T(8,128)(2,1)S(1)}, bf16[256,256]{1,0:T(8,128)(2,1)}, u32[]{:S(2)}) copy-start(bf16[256,256]{1,0:T(8,128)(2,1)} %wv.1) | copy-start | bytes 393220
  9.4 0.9 %copy-start.9 = (bf16[256,256]{1,0:T(8,128)(2,1)S(1)}, bf16[256,256]{1,0:T(8,128)(2,1)}, u32[]{:S(2)}) copy-start(bf16[256,256]{1,0:T(8,128)(2,1)} %wo.1) | copy-start | bytes 393220
  10.3 0.9 %copy-start.10 = (bf16[256,256]{1,0:T(8,128)(2,1)S(1)}, bf16[256,256]{1,0:T(8,128)(2,1)}, u32[]{:S(2)}) copy-start(bf16[256,256]{1,0:T(8,128)(2,1)} %wo_self.1) | copy-start | bytes 393220
  11.2 0.9 %copy-start.11 = (bf16[200,256]{1,0:T(8,128)(2,1)S(1)}, bf16[200,256]{1,0:T(8,128)(2,1)}, u32[]{:S(2)}) copy-start(bf16[200,256]{1,0:T(8,128)(2,1)} %query_pos.1) | copy-start | bytes 307204
  12.1 0.7 copy-start.12
  12.8 0.7 copy-start.13
  13.5 0.7 copy-start.14
where the time goes:
time: 69.2 us; the launch traced here: 68.8 us
  Pallas kernels  53.7 us (78%)
  local copies, waits for them, and re-layouts  15.1 us (22%)
    pallas_call x1, Pallas kernels, local(): pl.pallas_call(kernel, out_shape=jax.ShapeDtypeStruct((images, nq, width)...  53.7 us
    unnamed x31, local copies, waits for them, and re-layouts  15.1 us

commit v1 on v0

--- a/solution.py
+++ b/solution.py
@@ -50,10 +50,12 @@
 
 
 def kernel(
+    queries_in, query_pos_in, pixels_in, pixel_pos_in, masks_in, wq_in, wk_in, wv_in, wo_in, gain_cross_in, w_qkv_in,
+    wo_self_in, gain_self_in, w_in_in, w_out_in, gain_ffn_in,
+    out,
     queries, query_pos, pixels, pixel_pos, masks, wq, wk, wv, wo, gain_cross, w_qkv, wo_self, gain_self, w_in, w_out,
-    gain_ffn,
-    out,
-    wq_t, wv_t, eye, keys, values_t, query_t, bias, own_o, own_m,
+    gain_ffn, image_sem, early_sem, late_sem,
+    wq_t, wv_t, eye, keys, values_t, query_t, bias, scores, weights, own_o, own_m,
     p1o, p1m, r1o, r1m, p2o, p2m, r2o, r2m, p3o, p3m, r3o, r3m, att,
     s1, v1, s2, v2, s3, v3, s4, v4, s5, v5, s6, v6,
 ):
@@ -84,6 +86,34 @@
     for d in range(1, NZ):
         pl.semaphore_signal(barrier, inc=1, device_id=z_peer(d), device_id_type=MESH)
 
+    def image_loads(i):
+        pairs = ((pixels_in, pixels), (queries_in, queries), (masks_in, masks))
+        return [pltpu.make_async_copy(a.at[i], b.at[i], image_sem.at[i, k]) for k, (a, b) in enumerate(pairs)]
+
+    early = [
+        pltpu.make_async_copy(a, b, early_sem.at[k])
+        for k, (a, b) in enumerate(
+            ((wq_in, wq), (wv_in, wv), (wk_in, wk), (pixel_pos_in, pixel_pos), (query_pos_in, query_pos))
+        )
+    ]
+    late = [
+        pltpu.make_async_copy(a, b, late_sem.at[k])
+        for k, (a, b) in enumerate(
+            (
+                (wo_in, wo), (gain_cross_in, gain_cross), (w_qkv_in, w_qkv), (wo_self_in, wo_self),
+                (gain_self_in, gain_self), (w_in_in, w_in), (w_out_in, w_out), (gain_ffn_in, gain_ffn),
+            )
+        )
+    ]
+    for copy in early:
+        copy.start()
+    for group in (1 - core, core):
+        for j in range(NX):
+            for copy in image_loads(group * NX + lax.rem(x + j + 1, NX)):
+                copy.start()
+    for copy in late:
+        copy.start()
+
     def send(src, dst, send_sem, recv_sem, where):
         return pltpu.make_async_remote_copy(
             src_ref=src, dst_ref=dst, send_sem=send_sem, recv_sem=recv_sem, device_id=where, device_id_type=MESH
@@ -92,14 +122,18 @@
     rows = lax.broadcasted_iota(jnp.int32, (pix, pix), 0)
     cols = lax.broadcasted_iota(jnp.int32, (pix, pix), 1)
     eye[...] = jnp.where(rows == cols, 1.0, 0.0).astype(BF16)
-    wq_t[...] = dot_nt(eye[...], wq[...]).astype(BF16)
-    wv_t[...] = dot_nt(eye[...], wv[...]).astype(BF16)
     query_t[...] = jnp.zeros_like(query_t)
     bias[...] = jnp.zeros_like(bias)
     for h in range(HEADS):
         values_t[h, HEAD:, :] = jnp.ones((16, pix), BF16)
+    for copy in early:
+        copy.wait()
+    wq_t[...] = dot_nt(eye[...], wq[...]).astype(BF16)
+    wv_t[...] = dot_nt(eye[...], wv[...]).astype(BF16)
 
     def partial(i, put_o, m_ref):
+        for copy in image_loads(i):
+            copy.wait()
         one = pixels[i]
         key_in = (one.astype(F32) + pixel_pos[...].astype(F32)).astype(BF16)
         keys[...] = dot(key_in, wk[...]).astype(BF16)
@@ -123,11 +157,13 @@
                 parts.append(jnp.zeros((128 - lane - HEAD, LANES), BF16))
             one_head = jnp.concatenate(parts, axis=0)
             score = dot(keys[:, tile : tile + 128], one_head) * factor + bias[...]
-            top = jnp.max(score, axis=0, keepdims=True)
-            weight = jnp.exp2(score - top).astype(BF16)
-            both = dot(values_t[h], weight)
+            scores[h] = score
+            m_ref[h : h + 1, :] = jnp.max(score, axis=0, keepdims=True)
+        for h in range(HEADS):
+            weights[h] = jnp.exp2(scores[h] - m_ref[h : h + 1, :]).astype(BF16)
+        for h in range(HEADS):
+            both = dot(values_t[h], weights[h])
             put_o(h, both[:HEAD])
-            m_ref[h : h + 1, :] = top
             m_ref[HEADS + h : HEADS + h + 1, :] = both[HEAD : HEAD + 1]
         m_ref[HEADS:, :nq] = m_ref[HEADS:, :nq] * sign
 
@@ -226,6 +262,8 @@
         z_gather(d).wait()
 
     i_own = core * NX + x
+    for copy in late:
+        copy.wait()
     attended_t = att[...].reshape(width, LANES)
     cross = dot(attended_t, wo[...], ((0,), (0,)))[:nq]
     pos = query_pos[...].astype(F32)
@@ -251,27 +289,53 @@
         outs.append(gathered.astype(BF16))
     self_proj = dot(jnp.concatenate(outs, axis=1), wo_self[...])
     after_self = layer_norm(after_cross.astype(F32) + self_proj, gain_self[...]).astype(BF16)
-    hidden = jnp.maximum(dot(after_self, w_in[...]), 0.0).astype(BF16)
-    ffn = dot(hidden, w_out[...])
-    out[i_own] = layer_norm(after_self.astype(F32) + ffn, gain_ffn[...]).astype(BF16)
-
-    def x_out(d):
-        return send(out.at[i_own], out.at[i_own], s5.at[d - 1], v5.at[d - 1], x_peer(d))
-
-    def core_out(k):
-        i = core * NX + lax.rem(x - k + NX, NX)
-        return send(out.at[i], out.at[i], s6.at[k], v6.at[k], partner)
-
-    for d in (2, 1, 3):
-        x_out(d).start()
-    core_out(0).start()
-    for d in (1, 3, 2):
-        x_out(d).wait_recv()
-        core_out(d).start()
-    for d in (1, 2, 3):
-        x_out(d).wait_send()
-    for k in range(NX):
-        core_out(k).wait()
+    halves = (slice(0, 96), slice(96, nq))
+
+    def x_out(part, d, k):
+        rows = halves[part]
+        return send(out.at[i_own, rows], out.at[i_own, rows], s5.at[k], v5.at[k], x_peer(d))
+
+    def x_pass(part, d, k):
+        i = core * NX + lax.rem(x - d + NX, NX)
+        rows = halves[part]
+        return send(out.at[i, rows], out.at[i, rows], s5.at[k], v5.at[k], x_peer(d))
+
+    def core_out(part, back):
+        i = core * NX + lax.rem(x - back + NX, NX)
+        rows = halves[part]
+        k = 2 * back + part
+        return send(out.at[i, rows], out.at[i, rows], s6.at[k], v6.at[k], partner)
+
+    for part in range(2):
+        rows = halves[part]
+        hidden = jnp.maximum(dot(after_self[rows], w_in[...]), 0.0).astype(BF16)
+        ffn = dot(hidden, w_out[...])
+        out[i_own, rows] = layer_norm(after_self[rows].astype(F32) + ffn, gain_ffn[...]).astype(BF16)
+        x_out(part, 1, part).start()
+        x_out(part, NX - 1, 2 + part).start()
+        core_out(part, 0).start()
+    x_out(0, 1, 0).wait_recv()
+    x_pass(0, 1, 4).start()
+    core_out(0, 1).start()
+    x_out(0, NX - 1, 2).wait_recv()
+    core_out(0, NX - 1).start()
+    x_out(1, NX - 1, 3).wait_recv()
+    x_pass(1, NX - 1, 5).start()
+    core_out(1, NX - 1).start()
+    x_out(1, 1, 1).wait_recv()
+    core_out(1, 1).start()
+    x_pass(0, 1, 4).wait_recv()
+    core_out(0, 2).start()
+    x_pass(1, NX - 1, 5).wait_recv()
+    core_out(1, 2).start()
+    for part in range(2):
+        x_out(part, 1, part).wait_send()
+        x_out(part, NX - 1, 2 + part).wait_send()
+    x_pass(0, 1, 4).wait_send()
+    x_pass(1, NX - 1, 5).wait_send()
+    for part in range(2):
+        for back in range(NX):
+            core_out(part, back).wait()
 
 
 def local(
@@ -282,7 +346,14 @@
     pix = pixels.shape[1]
     dma = pltpu.SemaphoreType.DMA
     vmem = pltpu.VMEM
-    scratch = [
+    operands = (
+        queries, query_pos, pixels, pixel_pos, masks, wq_cross, wk_cross, wv_cross, wo_cross, gain_cross[None], w_qkv,
+        wo_self, gain_self[None], w_in, w_out, gain_ffn[None],
+    )
+    scratch = [vmem(a.shape, a.dtype) for a in operands] + [
+        dma((images, 3)),
+        dma((5,)),
+        dma((8,)),
         vmem((width, width), BF16),
         vmem((width, width), BF16),
         vmem((pix, pix), BF16),
@@ -290,6 +361,8 @@
         vmem((HEADS, HEAD + 16, pix), BF16),
         vmem((width, LANES), BF16),
         vmem((pix, LANES), F32),
+        vmem((HEADS, pix, LANES), F32),
+        vmem((HEADS, pix, LANES), BF16),
         vmem((width, LANES), F32),
         vmem((2 * HEADS, LANES), F32),
         vmem((NX, width, LANES), BF16),
@@ -313,25 +386,22 @@
         dma((NZ - 1, 2)),
         dma((NZ - 1,)),
         dma((NZ - 1,)),
-        dma((NX - 1,)),
-        dma((NX - 1,)),
-        dma((NX,)),
-        dma((NX,)),
+        dma((6,)),
+        dma((6,)),
+        dma((2 * NX,)),
+        dma((2 * NX,)),
     ]
     return pl.pallas_call(
         kernel,
         out_shape=jax.ShapeDtypeStruct((images, nq, width), BF16),
-        in_specs=[pl.BlockSpec(memory_space=pltpu.VMEM)] * 16,
+        in_specs=[pl.BlockSpec(memory_space=pltpu.HBM)] * 16,
         out_specs=pl.BlockSpec(memory_space=pltpu.VMEM),
         scratch_shapes=scratch,
         compiler_params=pltpu.CompilerParams(
-            collective_id=0, has_side_effects=True, vmem_limit_bytes=48 * 1024 * 1024
+            collective_id=0, has_side_effects=True, vmem_limit_bytes=67043328
         ),
         name="decoder_layer",
-    )(
-        queries, query_pos, pixels, pixel_pos, masks, wq_cross, wk_cross, wv_cross, wo_cross, gain_cross[None], w_qkv,
-        wo_self, gain_self[None], w_in, w_out, gain_ffn[None],
-    )
+    )(*operands)
 
 
 def solution(mesh):

time: 69.2 us -> 51.2 us (0.74)
  local copies, waits for them, and re-layouts: 15.1 us -> 2.09 us
  Pallas kernels: 53.7 us -> 48.3 us
    unnamed x31 -> x1, local copies, waits for them, and re-layouts: 15.1 us -> 2.09 us
    pallas_call x1, Pallas kernels: 53.7 us -> 48.3 us  [local(): pl.pallas_call(kernel, out_shape=jax.ShapeDtypeStruct((images, nq, width)...]
where the time goes in v1:
time: 51.2 us; the launch traced here: 50.4 us
  Pallas kernels  48.3 us (94%)
  local copies, waits for them, and re-layouts  2.09 us (4%)
    pallas_call x1, Pallas kernels, local(): pl.pallas_call(kernel, out_shape=jax.ShapeDtypeStruct((images, nq, width)...  48.3 us
    unnamed x1, local copies, waits for them, and re-layouts  2.09 us

profile of v1, /device:TPU:1, one launch (start us, length us, event | category | flops | bytes accessed | tf_op | source)
XLA Modules:
  0.0 50.4 jit_solution(14451475708597408794)
XLA Ops:
  0.0 48.3 %decoder_layer.1 = bf16[8,200,256]{2,1,0:T(8,128)(2,1)} custom-call(bf16[8,200,256]{2,1,0:T(8,128)(2,1)} %queries_in.1, bf16[200,256]{1,0:T(8,128)(2,1)} %query_pos_in.1, bf16[8,256,256]{2,1,0:T(8,128)(2,1)} %pixels_in.1, bf16[256,256]{1,0:T(8,128)(2,1)} %pixel_pos_in.1, s32[8,200,256]{2,1,0:T(8,128)} %masks_in.1, bf16[256,256]{1,0:T(8,128)(2,1)} %wq_in.1, ...), custom_call_target="tpu_custom_call" | custom-call | tf_op jit(solution)/shard_map/decoder_layer/pallas_call | solution.py:394
  48.3 2.1 %copy.18 = bf16[8,200,256]{2,1,0:T(8,128)(2,1)} copy(bf16[8,200,256]{2,1,0:T(8,128)(2,1)} %decoder_layer.1) | data formatting | bytes 1638400

commit v2 on v1

--- a/solution.py
+++ b/solution.py
@@ -55,9 +55,10 @@
     out,
     queries, query_pos, pixels, pixel_pos, masks, wq, wk, wv, wo, gain_cross, w_qkv, wo_self, gain_self, w_in, w_out,
     gain_ffn, image_sem, early_sem, late_sem,
-    wq_t, wv_t, eye, keys, values_t, query_t, bias, scores, weights, own_o, own_m,
+    wq_t, wv_t, eye, keys_a, values_a, query_a, bias_a, keys_b, values_b, query_b, bias_b, scores, weights, own_o, own_m,
     p1o, p1m, r1o, r1m, p2o, p2m, r2o, r2m, p3o, p3m, r3o, r3m, att,
-    s1, v1, s2, v2, s3, v3, s4, v4, s5, v5, s6, v6,
+    mine_out, around,
+    s1, v1, s2, v2, s3, v3, s4, v4, s5, v5, s6, v6, store_sem,
 ):
     nq = queries.shape[1]
     width = queries.shape[2]
@@ -79,13 +80,6 @@
 
     partner = at(x, z, 1 - core)
 
-    barrier = pltpu.get_barrier_semaphore()
-    pl.semaphore_signal(barrier, inc=1, device_id=partner, device_id_type=MESH)
-    for d in range(1, NX):
-        pl.semaphore_signal(barrier, inc=1, device_id=x_peer(d), device_id_type=MESH)
-    for d in range(1, NZ):
-        pl.semaphore_signal(barrier, inc=1, device_id=z_peer(d), device_id_type=MESH)
-
     def image_loads(i):
         pairs = ((pixels_in, pixels), (queries_in, queries), (masks_in, masks))
         return [pltpu.make_async_copy(a.at[i], b.at[i], image_sem.at[i, k]) for k, (a, b) in enumerate(pairs)]
@@ -107,12 +101,17 @@
     ]
     for copy in early:
         copy.start()
-    for group in (1 - core, core):
-        for j in range(NX):
+    for j in range(NX):
+        for group in (1 - core, core):
             for copy in image_loads(group * NX + lax.rem(x + j + 1, NX)):
                 copy.start()
-    for copy in late:
-        copy.start()
+
+    barrier = pltpu.get_barrier_semaphore()
+    pl.semaphore_signal(barrier, inc=1, device_id=partner, device_id_type=MESH)
+    for d in range(1, NX):
+        pl.semaphore_signal(barrier, inc=1, device_id=x_peer(d), device_id_type=MESH)
+    for d in range(1, NZ):
+        pl.semaphore_signal(barrier, inc=1, device_id=z_peer(d), device_id_type=MESH)
 
     def send(src, dst, send_sem, recv_sem, where):
         return pltpu.make_async_remote_copy(
@@ -122,30 +121,45 @@
     rows = lax.broadcasted_iota(jnp.int32, (pix, pix), 0)
     cols = lax.broadcasted_iota(jnp.int32, (pix, pix), 1)
     eye[...] = jnp.where(rows == cols, 1.0, 0.0).astype(BF16)
-    query_t[...] = jnp.zeros_like(query_t)
-    bias[...] = jnp.zeros_like(bias)
-    for h in range(HEADS):
-        values_t[h, HEAD:, :] = jnp.ones((16, pix), BF16)
+    theirs = (keys_a, values_a, query_a, bias_a)
+    ours = (keys_b, values_b, query_b, bias_b)
+    for _, values_t, query_t, bias in (theirs, ours):
+        query_t[...] = jnp.zeros_like(query_t)
+        bias[:pix] = jnp.zeros((pix, LANES), F32)
+        bias[pix:] = jnp.ones((8, LANES), F32)
+        for h in range(HEADS):
+            values_t[h, HEAD:, :] = jnp.ones((16, pix), BF16)
     for copy in early:
         copy.wait()
     wq_t[...] = dot_nt(eye[...], wq[...]).astype(BF16)
     wv_t[...] = dot_nt(eye[...], wv[...]).astype(BF16)
 
-    def partial(i, put_o, m_ref):
-        for copy in image_loads(i):
-            copy.wait()
-        one = pixels[i]
-        key_in = (one.astype(F32) + pixel_pos[...].astype(F32)).astype(BF16)
-        keys[...] = dot(key_in, wk[...]).astype(BF16)
-        v_t = dot_nt(wv_t[...], one).astype(BF16)
-        for h in range(HEADS):
-            values_t[h, :HEAD, :] = v_t[h * HEAD : (h + 1) * HEAD, :]
-        query_in = (queries[i].astype(F32) + query_pos[...].astype(F32)).astype(BF16)
-        query_t[:, :nq] = dot_nt(wq_t[...], query_in).astype(BF16)
-        mask_t = dot_nt(eye[...], masks[i].astype(F32).astype(BF16))
-        count = jnp.sum(mask_t, axis=0, keepdims=True)
-        bias[:, :nq] = jnp.where((mask_t > 0.5) | (count == 0.0), 0.0, FAR)
-        sign = jnp.where(count == 0.0, -1.0, 1.0)
+    def prepare(i, bufs):
+        keys, values_t, query_t, bias = bufs
+
+        def key_piece():
+            key_in = (pixels[i].astype(F32) + pixel_pos[...].astype(F32)).astype(BF16)
+            keys[...] = dot(key_in, wk[...]).astype(BF16)
+
+        def value_piece():
+            v_t = dot_nt(wv_t[...], pixels[i]).astype(BF16)
+            for h in range(HEADS):
+                values_t[h, :HEAD, :] = v_t[h * HEAD : (h + 1) * HEAD, :]
+
+        def query_piece():
+            query_in = (queries[i].astype(F32) + query_pos[...].astype(F32)).astype(BF16)
+            query_t[:, :nq] = dot_nt(wq_t[...], query_in).astype(BF16)
+
+        def mask_piece():
+            mask_t = dot_nt(eye[...], masks[i].astype(F32).astype(BF16))
+            count = jnp.sum(mask_t, axis=0, keepdims=True)
+            bias[:pix, :nq] = jnp.where((mask_t > 0.5) | (count == 0.0), 0.0, FAR)
+            bias[pix : pix + 1, :nq] = jnp.where(count == 0.0, -1.0, 1.0)
+
+        return [key_piece, value_piece, query_piece, mask_piece]
+
+    def attend(bufs, put_o, m_ref, pieces):
+        keys, values_t, query_t, bias = bufs
         for h in range(HEADS):
             tile = (h // 4) * 128
             lane = (h % 4) * HEAD
@@ -156,69 +170,94 @@
             if lane + HEAD < 128:
                 parts.append(jnp.zeros((128 - lane - HEAD, LANES), BF16))
             one_head = jnp.concatenate(parts, axis=0)
-            score = dot(keys[:, tile : tile + 128], one_head) * factor + bias[...]
+            score = dot(keys[:, tile : tile + 128], one_head) * factor + bias[:pix]
             scores[h] = score
             m_ref[h : h + 1, :] = jnp.max(score, axis=0, keepdims=True)
+            if pieces and h % 2 == 1:
+                pieces[h // 2]()
         for h in range(HEADS):
             weights[h] = jnp.exp2(scores[h] - m_ref[h : h + 1, :]).astype(BF16)
         for h in range(HEADS):
             both = dot(values_t[h], weights[h])
             put_o(h, both[:HEAD])
-            m_ref[HEADS + h : HEADS + h + 1, :] = both[HEAD : HEAD + 1]
-        m_ref[HEADS:, :nq] = m_ref[HEADS:, :nq] * sign
-
-    def first(j, carry):
-        i = (1 - core) * NX + lax.rem(x + j + 1, NX)
+            m_ref[HEADS + h : HEADS + h + 1, :] = both[HEAD : HEAD + 1] * bias[pix : pix + 1]
+
+    def turn(j, cc):
+        first = j // (NX - 1)
+        second = lax.rem(j, 2) * (1 - first)
+        return 2 * (1 - (j + 2) // (NX - 1)) + (1 + 2 * cc) * second + (3 - 2 * cc) * (j // 2) * (1 - first)
+
+    def image(j, cc):
+        return cc * NX + lax.rem(x + turn(j, cc), NX)
+
+    def arrived(i):
+        for copy in image_loads(i):
+            copy.wait()
+
+    arrived(image(0, 1 - core))
+    for piece in prepare(image(0, 1 - core), theirs):
+        piece()
+
+    def step(j, carry):
+        far = turn(j, core)
 
         def put(h, value):
             p1o[j, h * HEAD : (h + 1) * HEAD, :] = value.astype(BF16)
 
-        partial(i, put, p1m.at[j])
+        arrived(image(j, core))
+        attend(theirs, put, p1m.at[j], prepare(image(j, core), ours))
 
         @pl.when(j == 0)
         def _():
             pl.semaphore_wait(barrier, NX + NZ - 1)
-
-        send(p1o.at[j], r1o.at[j], s1.at[j, 0], v1.at[j, 0], partner).start()
-        send(p1m.at[j], r1m.at[j], s1.at[j, 1], v1.at[j, 1], partner).start()
-        return carry
-
-    lax.fori_loop(0, NX, first, 0)
-
-    def second(j, carry):
-        i = core * NX + lax.rem(x + j + 1, NX)
-
-        def put(h, value):
-            own_o[h * HEAD : (h + 1) * HEAD, :] = value
-
-        partial(i, put, own_m)
+            for copy in late:
+                copy.start()
+
         a = send(p1o.at[j], r1o.at[j], s1.at[j, 0], v1.at[j, 0], partner)
         b = send(p1m.at[j], r1m.at[j], s1.at[j, 1], v1.at[j, 1], partner)
+        a.start()
+        b.start()
+
+        def put_own(h, value):
+            own_o[h * HEAD : (h + 1) * HEAD, :] = value
+
+        following = image(jnp.minimum(j + 1, NX - 1), 1 - core)
+
+        @pl.when(j < NX - 1)
+        def _():
+            arrived(following)
+
+        attend(ours, put_own, own_m, prepare(following, theirs))
         a.wait()
         b.wait()
         top, total, scales = merge([own_m[:HEADS], r1m[j, :HEADS]], [own_m[HEADS:], r1m[j, HEADS:]])
-        p2m[j, :HEADS] = top
-        p2m[j, HEADS:] = total
+        p2m[far, :HEADS] = top
+        p2m[far, HEADS:] = total
         for h in range(HEADS):
             part = slice(h * HEAD, (h + 1) * HEAD)
             folded = own_o[part] * scales[0][h : h + 1] + r1o[j, part].astype(F32) * scales[1][h : h + 1]
-            p2o[j, part] = folded.astype(BF16)
+            p2o[far, part] = folded.astype(BF16)
 
         @pl.when(j < NX - 1)
         def _():
-            to = x_peer(j + 1)
-            send(p2o.at[j], r2o.at[j], s2.at[j, 0], v2.at[j, 0], to).start()
-            send(p2m.at[j], r2m.at[j], s2.at[j, 1], v2.at[j, 1], to).start()
+            for copy in x_send(far):
+                copy.start()
 
         return carry
 
-    lax.fori_loop(0, NX, second, 0)
-
-    mine = NX - 1
-    for j in range(NX - 1):
-        to = x_peer(j + 1)
-        send(p2o.at[j], r2o.at[j], s2.at[j, 0], v2.at[j, 0], to).wait()
-        send(p2m.at[j], r2m.at[j], s2.at[j, 1], v2.at[j, 1], to).wait()
+    def x_send(far):
+        k = far - 1
+        return (
+            send(p2o.at[far], r2o.at[k], s2.at[k, 0], v2.at[k, 0], x_peer(far)),
+            send(p2m.at[far], r2m.at[k], s2.at[k, 1], v2.at[k, 1], x_peer(far)),
+        )
+
+    lax.fori_loop(0, NX, step, 0)
+
+    mine = 0
+    for far in range(1, NX):
+        for copy in x_send(far):
+            copy.wait()
     tops = [p2m[mine, :HEADS]] + [r2m[j, :HEADS] for j in range(NX - 1)]
     totals = [p2m[mine, HEADS:]] + [r2m[j, HEADS:] for j in range(NX - 1)]
     top, total, scales = merge(tops, totals)
@@ -228,8 +267,9 @@
         for j in range(NX - 1):
             folded = folded + r2o[j, part].astype(F32) * scales[j + 1][h : h + 1]
         p3o[h] = folded.astype(BF16)
-        p3m[h, 0:1] = top[h : h + 1]
-        p3m[h, 1:2] = total[h : h + 1]
+        for k, value in enumerate((top, total)):
+            p3m[h, 2 * k : 2 * k + 1] = value[h : h + 1, :128]
+            p3m[h, 2 * k + 1 : 2 * k + 2] = value[h : h + 1, 128:]
 
     def z_send(d):
         h = lax.rem(z + d, NZ)
@@ -245,8 +285,12 @@
     for d in order[::-1]:
         for copy in z_send(d):
             copy.wait()
-    tops = [p3m[z, 0:1]] + [r3m[d, 0:1] for d in range(NZ - 1)]
-    totals = [p3m[z, 1:2]] + [r3m[d, 1:2] for d in range(NZ - 1)]
+
+    def wide(ref, k, which):
+        return jnp.concatenate([ref[k, 2 * which : 2 * which + 1], ref[k, 2 * which + 1 : 2 * which + 2]], axis=1)
+
+    tops = [wide(p3m, z, 0)] + [wide(r3m, d, 0) for d in range(NZ - 1)]
+    totals = [wide(p3m, z, 1)] + [wide(r3m, d, 1) for d in range(NZ - 1)]
     top, total, scales = merge(tops, totals)
     folded = p3o[z].astype(F32) * scales[0]
     for d in range(NZ - 1):
@@ -291,51 +335,59 @@
     after_self = layer_norm(after_cross.astype(F32) + self_proj, gain_self[...]).astype(BF16)
     halves = (slice(0, 96), slice(96, nq))
 
-    def x_out(part, d, k):
+    def x_out(part, d):
         rows = halves[part]
-        return send(out.at[i_own, rows], out.at[i_own, rows], s5.at[k], v5.at[k], x_peer(d))
-
-    def x_pass(part, d, k):
-        i = core * NX + lax.rem(x - d + NX, NX)
+        k = 2 * (d // 2) + part
+        return send(mine_out.at[rows], around.at[d - 1, rows], s5.at[k], v5.at[k], x_peer(d))
+
+    def x_pass(part):
         rows = halves[part]
-        return send(out.at[i, rows], out.at[i, rows], s5.at[k], v5.at[k], x_peer(d))
-
-    def core_out(part, back):
-        i = core * NX + lax.rem(x - back + NX, NX)
+        back, d = ((1, 1), (NX - 1, NX - 1))[part]
+        return send(around.at[back - 1, rows], around.at[1, rows], s5.at[4 + part], v5.at[4 + part], x_peer(d))
+
+    def finish(part, back):
         rows = halves[part]
         k = 2 * back + part
-        return send(out.at[i, rows], out.at[i, rows], s6.at[k], v6.at[k], partner)
+        i = core * NX + lax.rem(x - back + NX, NX)
+        source = mine_out.at[rows] if back == 0 else around.at[back - 1, rows]
+        return (
+            pltpu.make_async_copy(source, out.at[i, rows], store_sem.at[k]),
+            send(source, out.at[i, rows], s6.at[k], v6.at[k], partner),
+        )
+
+    def pass_on(part, back):
+        for copy in finish(part, back)[::-1]:
+            copy.start()
 
     for part in range(2):
         rows = halves[part]
         hidden = jnp.maximum(dot(after_self[rows], w_in[...]), 0.0).astype(BF16)
         ffn = dot(hidden, w_out[...])
-        out[i_own, rows] = layer_norm(after_self[rows].astype(F32) + ffn, gain_ffn[...]).astype(BF16)
-        x_out(part, 1, part).start()
-        x_out(part, NX - 1, 2 + part).start()
-        core_out(part, 0).start()
-    x_out(0, 1, 0).wait_recv()
-    x_pass(0, 1, 4).start()
-    core_out(0, 1).start()
-    x_out(0, NX - 1, 2).wait_recv()
-    core_out(0, NX - 1).start()
-    x_out(1, NX - 1, 3).wait_recv()
-    x_pass(1, NX - 1, 5).start()
-    core_out(1, NX - 1).start()
-    x_out(1, 1, 1).wait_recv()
-    core_out(1, 1).start()
-    x_pass(0, 1, 4).wait_recv()
-    core_out(0, 2).start()
-    x_pass(1, NX - 1, 5).wait_recv()
-    core_out(1, 2).start()
+        mine_out[rows] = layer_norm(after_self[rows].astype(F32) + ffn, gain_ffn[...]).astype(BF16)
+        x_out(part, 1).start()
+        x_out(part, NX - 1).start()
+        pass_on(part, 0)
+    x_out(0, 1).wait_recv()
+    x_pass(0).start()
+    pass_on(0, 1)
+    x_out(0, NX - 1).wait_recv()
+    pass_on(0, NX - 1)
+    x_out(1, NX - 1).wait_recv()
+    x_pass(1).start()
+    pass_on(1, NX - 1)
+    x_out(1, 1).wait_recv()
+    pass_on(1, 1)
+    x_pass(0).wait_recv()
+    pass_on(0, 2)
+    x_pass(1).wait_recv()
+    pass_on(1, 2)
     for part in range(2):
-        x_out(part, 1, part).wait_send()
-        x_out(part, NX - 1, 2 + part).wait_send()
-    x_pass(0, 1, 4).wait_send()
-    x_pass(1, NX - 1, 5).wait_send()
-    for part in range(2):
+        x_out(part, 1).wait_send()
+        x_out(part, NX - 1).wait_send()
+        x_pass(part).wait_send()
         for back in range(NX):
-            core_out(part, back).wait()
+            for copy in finish(part, back):
+                copy.wait()
 
 
 def local(
@@ -360,7 +412,11 @@
         vmem((pix, width), BF16),
         vmem((HEADS, HEAD + 16, pix), BF16),
         vmem((width, LANES), BF16),
-        vmem((pix, LANES), F32),
+        vmem((pix + 8, LANES), F32),
+        vmem((pix, width), BF16),
+        vmem((HEADS, HEAD + 16, pix), BF16),
+        vmem((width, LANES), BF16),
+        vmem((pix + 8, LANES), F32),
         vmem((HEADS, pix, LANES), F32),
         vmem((HEADS, pix, LANES), BF16),
         vmem((width, LANES), F32),
@@ -374,10 +430,12 @@
         vmem((NX - 1, width, LANES), BF16),
         vmem((NX - 1, 2 * HEADS, LANES), F32),
         vmem((NZ, HEAD, LANES), BF16),
-        vmem((NZ, 8, LANES), F32),
+        vmem((NZ, 8, 128), F32),
         vmem((NZ - 1, HEAD, LANES), BF16),
-        vmem((NZ - 1, 8, LANES), F32),
+        vmem((NZ - 1, 8, 128), F32),
         vmem((NZ, HEAD, LANES), BF16),
+        vmem((nq, width), BF16),
+        vmem((NX - 1, nq, width), BF16),
         dma((NX, 2)),
         dma((NX, 2)),
         dma((NX - 1, 2)),
@@ -390,12 +448,13 @@
         dma((6,)),
         dma((2 * NX,)),
         dma((2 * NX,)),
+        dma((2 * NX,)),
     ]
     return pl.pallas_call(
         kernel,
         out_shape=jax.ShapeDtypeStruct((images, nq, width), BF16),
         in_specs=[pl.BlockSpec(memory_space=pltpu.HBM)] * 16,
-        out_specs=pl.BlockSpec(memory_space=pltpu.VMEM),
+        out_specs=pl.BlockSpec(memory_space=pltpu.HBM),
         scratch_shapes=scratch,
         compiler_params=pltpu.CompilerParams(
             collective_id=0, has_side_effects=True, vmem_limit_bytes=67043328

time: 51.2 us -> 45.3 us (0.88); the launches traced: 50.4 us -> 45.2 us
  Pallas kernels: 48.3 us -> 43.1 us
    pallas_call x1, Pallas kernels: 48.3 us -> 43.1 us  [local(): pl.pallas_call(kernel, out_shape=jax.ShapeDtypeStruct((images, nq, width)...]
where the time goes in v2:
time: 45.3 us; the launch traced here: 45.2 us
  Pallas kernels  43.1 us (95%)
  local copies, waits for them, and re-layouts  2.09 us (5%)
    pallas_call x1, Pallas kernels, local(): pl.pallas_call(kernel, out_shape=jax.ShapeDtypeStruct((images, nq, width)...  43.1 us
    unnamed x1, local copies, waits for them, and re-layouts  2.09 us

profile of v2, /device:TPU:1, one launch (start us, length us, event | category | flops | bytes accessed | tf_op | source)
XLA Modules:
  0.0 45.2 jit_solution(7465019809749408613)
XLA Ops:
  0.0 43.1 %decoder_layer.1 = bf16[8,200,256]{2,1,0:T(8,128)(2,1)} custom-call(bf16[8,200,256]{2,1,0:T(8,128)(2,1)} %queries_in.1, bf16[200,256]{1,0:T(8,128)(2,1)} %query_pos_in.1, bf16[8,256,256]{2,1,0:T(8,128)(2,1)} %pixels_in.1, bf16[256,256]{1,0:T(8,128)(2,1)} %pixel_pos_in.1, s32[8,200,256]{2,1,0:T(8,128)} %masks_in.1, bf16[256,256]{1,0:T(8,128)(2,1)} %wq_in.1, ...), custom_call_target="tpu_custom_call" | custom-call | tf_op jit(solution)/shard_map/decoder_layer/pallas_call | solution.py:453
  43.1 2.1 %copy.18 = bf16[8,200,256]{2,1,0:T(8,128)(2,1)} copy(bf16[8,200,256]{2,1,0:T(8,128)(2,1)} %decoder_layer.1) | data formatting | bytes 1638400

commit v3 on v2

--- a/solution.py
+++ b/solution.py
@@ -101,10 +101,20 @@
     ]
     for copy in early:
         copy.start()
-    for j in range(NX):
-        for group in (1 - core, core):
-            for copy in image_loads(group * NX + lax.rem(x + j + 1, NX)):
-                copy.start()
+    def turn(j, cc):
+        first = j // (NX - 1)
+        second = lax.rem(j, 2) * (1 - first)
+        return 2 * (1 - (j + 2) // (NX - 1)) + (1 + 2 * cc) * second + (3 - 2 * cc) * (j // 2) * (1 - first)
+
+    def image(j, cc):
+        return cc * NX + lax.rem(x + turn(j, cc), NX)
+
+    def fetch(j, cc):
+        for copy in image_loads(image(j, cc)):
+            copy.start()
+
+    fetch(0, 1 - core)
+    fetch(0, core)
 
     barrier = pltpu.get_barrier_semaphore()
     pl.semaphore_signal(barrier, inc=1, device_id=partner, device_id_type=MESH)
@@ -131,6 +141,9 @@
             values_t[h, HEAD:, :] = jnp.ones((16, pix), BF16)
     for copy in early:
         copy.wait()
+    for j in range(1, NX):
+        fetch(j, 1 - core)
+        fetch(j, core)
     wq_t[...] = dot_nt(eye[...], wq[...]).astype(BF16)
     wv_t[...] = dot_nt(eye[...], wv[...]).astype(BF16)
 
@@ -181,14 +194,6 @@
             both = dot(values_t[h], weights[h])
             put_o(h, both[:HEAD])
             m_ref[HEADS + h : HEADS + h + 1, :] = both[HEAD : HEAD + 1] * bias[pix : pix + 1]
-
-    def turn(j, cc):
-        first = j // (NX - 1)
-        second = lax.rem(j, 2) * (1 - first)
-        return 2 * (1 - (j + 2) // (NX - 1)) + (1 + 2 * cc) * second + (3 - 2 * cc) * (j // 2) * (1 - first)
-
-    def image(j, cc):
-        return cc * NX + lax.rem(x + turn(j, cc), NX)
 
     def arrived(i):
         for copy in image_loads(i):

time: 45.3 us -> 45.3 us (level)
  no operation moved by 1% of the time
where the time goes in v3:
time: 45.3 us; the launch traced here: 45.2 us
  Pallas kernels  43.1 us (95%)
  local copies, waits for them, and re-layouts  2.09 us (5%)
    pallas_call x1, Pallas kernels, local(): pl.pallas_call(kernel, out_shape=jax.ShapeDtypeStruct((images, nq, width)...  43.1 us
    unnamed x1, local copies, waits for them, and re-layouts  2.09 us

profile of v3, /device:TPU:1, one launch (start us, length us, event | category | flops | bytes accessed | tf_op | source)
XLA Modules:
  0.0 45.2 jit_solution(12560299317491190947)
XLA Ops:
  0.0 43.1 %decoder_layer.1 = bf16[8,200,256]{2,1,0:T(8,128)(2,1)} custom-call(bf16[8,200,256]{2,1,0:T(8,128)(2,1)} %queries_in.1, bf16[200,256]{1,0:T(8,128)(2,1)} %query_pos_in.1, bf16[8,256,256]{2,1,0:T(8,128)(2,1)} %pixels_in.1, bf16[256,256]{1,0:T(8,128)(2,1)} %pixel_pos_in.1, s32[8,200,256]{2,1,0:T(8,128)} %masks_in.1, bf16[256,256]{1,0:T(8,128)(2,1)} %wq_in.1, ...), custom_call_target="tpu_custom_call" | custom-call | tf_op jit(solution)/shard_map/decoder_layer/pallas_call | solution.py:458
  43.1 2.1 %copy.18 = bf16[8,200,256]{2,1,0:T(8,128)(2,1)} copy(bf16[8,200,256]{2,1,0:T(8,128)(2,1)} %decoder_layer.1) | data formatting | bytes 1638400
